TPU v7x, 16 devices: a 4x2x1 block of a 4x4x8 slice. The times are simulated.
16 devices in a mesh: dp: 4 (over y, z, core), tp: 4 (over x).
Axes of the slice: x: 4, y: 2, z: 1, core: 2. Of those that a mesh axis runs over, the one named last changes fastest.
The devices are a block of a 4x4x8 slice.
Arguments:
- x: bfloat16 [8192, 5120], P('dp'), parts along dimension 0
- w_gate: bfloat16 [5120, 17920], P(None, 'tp')
- w_up: bfloat16 [5120, 17920], P(None, 'tp')
- w_down: bfloat16 [17920, 5120], P('tp')
Outputs:
- output: bfloat16 [8192, 5120], P('dp'), parts along dimension 0
There are 4 independent parts. A program takes and returns all parts, laid end to end along the dimension named above; an argument that names none is the same for every part.
All inputs are finite; a program needn't handle non-finite values.
Results may differ from a plain program's by a relative error of at most 0.016.
Values are sent between devices in bfloat16 or wider.
A program may use at most 768 MiB of HBM per device.

v0:
```python
import jax
import jax.numpy as jnp
from jax import lax
from jax.sharding import PartitionSpec as P


def solution(mesh):
    def step(x, w_gate, w_up, w_down):
        gate = jnp.dot(x, w_gate, preferred_element_type=jnp.float32)
        up = jnp.dot(x, w_up, preferred_element_type=jnp.float32)
        hidden = (jax.nn.silu(gate) * up).astype(jnp.bfloat16)
        term = jnp.dot(hidden, w_down, preferred_element_type=jnp.float32).astype(jnp.bfloat16)
        return lax.psum(term, "tp")

    return jax.shard_map(
        step,
        mesh=mesh,
        in_specs=(P("dp", None), P(None, "tp"), P(None, "tp"), P("tp", None)),
        out_specs=P("dp", None),
        check_vma=False,
    )
```

profile of v0, /device:TPU:112, one launch (start us, length us, event | category | flops | bytes accessed | tf_op | source)
XLA Modules:
  0.0 725.5 jit_solution(6291786684780042269)
XLA Ops:
  6.5 0.0 all-reduce.2.cloned.1.call-start
  6.6 112.5 %fusion = f32[2048,4480]{1,0:T(8,128)} fusion(bf16[2048,5120]{1,0:T(8,128)(2,1)} %param.4, bf16[5120,4480]{1,0:T(8,128)(2,1)} %param.5), kind=kOutput, calls=%fused_computation.2 | convolution fusion | flops 93952409600 | bytes 103546880 | tf_op jit(solution)/shard_map/dot_general | solution.py:9
  119.0 117.3 %multiply_convert_fusion = bf16[2048,4480]{1,0:T(8,128)(2,1)} fusion(f32[2048,4480]{1,0:T(8,128)} %fusion, bf16[2048,5120]{1,0:T(8,128)(2,1)} %param.4, bf16[5120,4480]{1,0:T(8,128)(2,1)} %param.6), kind=kOutput, calls=%fused_computation | convolution fusion | flops 94007459840 | bytes 121896960 | tf_op jit(solution)/shard_map/dot_general | solution.py:10
  236.3 107.1 %convolution_convert_fusion = bf16[2048,5120]{1,0:T(8,128)(2,1)} fusion(bf16[2048,4480]{1,0:T(8,128)(2,1)} %multiply_convert_fusion, bf16[4480,5120]{1,0:T(8,128)(2,1)} %param.7), kind=kOutput, calls=%fused_computation.1 | convolution fusion | flops 93962895360 | bytes 85196800 | tf_op jit(solution)/shard_map/dot_general | solution.py:12
  343.4 0.1 all-reduce.2.cloned.1.call-update
  343.5 357.9 %all-reduce.2.cloned.1.call-done = bf16[2048,5120]{1,0:T(8,128)(2,1)} async-done(((bf16[2048,5120]{1,0:T(8,128)(2,1)}), bf16[2048,5120]{1,0:T(8,128)(2,1)}) %all-reduce.2.cloned.1.call-update) | async-done | bytes 20971536 | tf_op jit(solution)/shard_map/psum | solution.py:13
  701.3 17.3 %copy.6 = bf16[2048,5120]{1,0:T(8,128)(2,1)} copy(bf16[2048,5120]{1,0:T(8,128)(2,1)} %all-reduce.2.cloned.1.call-done) | data formatting | bytes 41943040
Async XLA Ops:
  6.5 694.8 %all-reduce.2.cloned.1.call-start = ((), (), s32[]{:S(2)}) async-start(), calls=%async_computation | async-start | bytes 41943040 | tf_op jit(solution)/shard_map/psum | solution.py:13
Sparse Core Ops, SparseCore 0:
  343.6 357.6 all-reduce.1
where the time goes:
time: 726 us; the launch traced here: 725 us
  waiting for transfers between devices  358 us (49%)
  matrix products  337 us (46%)
  local copies, waits for them, and re-layouts  17.3 us (2%)
  between operations  13.4 us (2%)
    psum x1, waiting for transfers between devices, step(): return lax.psum(term, 'tp')  358 us
    dot_general x1, matrix products, step(): up = jnp.dot(x, w_up, preferred_element_type=jnp.float32)  117 us
    dot_general x1, matrix products, step(): gate = jnp.dot(x, w_gate, preferred_element_type=jnp.float32)  112 us
    dot_general x1, matrix products, step(): jnp.dot(hidden, w_down, preferred_element_type=jnp.float32)  107 us
    unnamed x1, local copies, waits for them, and re-layouts  17.3 us
  transfers between devices with their start and end apart: 1, of which 1 were waited for; matrix products, arithmetic and copies ran while one was open for 0% of the time, Pallas kernels for 0%

commit v1 on v0

v1 whole, which is shorter than its diff:
```python
import functools

import jax
import jax.numpy as jnp
from jax import lax
from jax.experimental import pallas as pl
from jax.experimental.pallas import tpu as pltpu
from jax.sharding import PartitionSpec as P

MESH = pl.DeviceIdType.MESH
F32, BF16 = jnp.float32, jnp.bfloat16

SMALL, BIG = 2, 3
UP, DOWN = 7, 4
STEPS = UP + DOWN
HOPS = 6
EVENTS = HOPS * DOWN


def block_kernel(
    n, x_hbm, wg_hbm, wu_hbm, wd_hbm, y_hbm,
    w_buf, x_buf, hid, term, stage, got,
    w_sem, x_sem, o_sem, send_sem, recv_sem,
):
    rows, dim = x_hbm.shape
    units = wg_hbm.shape[1]
    wide = dim // DOWN
    half = wide // 2
    tile = units // UP
    few = rows // 8
    many = 2 * few

    me = lax.axis_index("tp")
    group = lax.axis_index("dp")
    peers = (lax.rem(me + 1, n), lax.rem(me + n - 1, n))

    barrier = pltpu.get_barrier_semaphore()
    for peer in peers:
        pl.semaphore_signal(barrier, inc=1, device_id=(group, peer), device_id_type=MESH)

    def up_copies(s, slot):
        cols = pl.ds(pl.multiple_of(s * tile, 128), tile)
        return (
            pltpu.make_async_copy(wg_hbm.at[:, cols], w_buf.at[slot, :, pl.ds(0, tile)], w_sem.at[slot, 0]),
            pltpu.make_async_copy(wu_hbm.at[:, cols], w_buf.at[slot, :, pl.ds(tile, tile)], w_sem.at[slot, 1]),
        )

    def down_copy(s, slot):
        cols = pl.ds(pl.multiple_of(s * wide, 128), wide)
        return pltpu.make_async_copy(wd_hbm.at[:, cols], w_buf.at[slot, pl.ds(0, units), pl.ds(0, wide)], w_sem.at[slot, 0])

    def start_up(s, slot):
        for copy in up_copies(s, slot):
            copy.start()

    def x_copy(row, count):
        return pltpu.make_async_copy(x_hbm.at[pl.ds(pl.multiple_of(row, 16), count)], x_buf.at[pl.ds(0, count)], x_sem)

    def block_at(d, k):
        return lax.rem(me + 2 * n - 1 - k, n) if d == 0 else lax.rem(me + 1 + k, n)

    def y_at(d, u, k, row, high):
        start = pl.multiple_of(row + block_at(d, k) * high, 16)
        return y_hbm.at[pl.ds(start, high), pl.ds(pl.multiple_of(u * wide + d * half, 128), half)]

    def hop(d, u, k, src, dst):
        return pltpu.make_async_remote_copy(
            src_ref=src, dst_ref=dst,
            send_sem=send_sem.at[d, u, k], recv_sem=recv_sem.at[d, u, k],
            device_id=(group, peers[d]), device_id_type=MESH,
        )

    def partial_hop(d, u, k, high):
        return hop(d, u, k, stage.at[d, u, lax.rem(k, 2), pl.ds(0, high)], got.at[d, u, k, pl.ds(0, high)])

    def own_copy(d, u, row, high):
        return pltpu.make_async_copy(stage.at[d, u, 1, pl.ds(0, high)], y_at(d, u, n - 1, row, high), o_sem.at[d, u])

    def mine(d, u, k, high):
        return term[u, d, pl.ds(pl.multiple_of(block_at(d, k) * high, 16), high), :]

    def first_hop(u, high):
        for d in (0, 1):
            stage[d, u, 0, pl.ds(0, high), :] = mine(d, u, 0, high).astype(BF16)
            partial_hop(d, u, 0, high).start()

    def event(e, row, high):
        k, u = e // DOWN + 1, lax.rem(e, DOWN)

        @pl.when(k < n)
        def _():
            for d in (0, 1):
                partial_hop(d, u, k - 1, high).wait()
                total = got[d, u, k - 1, pl.ds(0, high), :].astype(F32) + mine(d, u, k, high)
                stage[d, u, lax.rem(k, 2), pl.ds(0, high), :] = total.astype(BF16)

                @pl.when(k < n - 1)
                def _():
                    partial_hop(d, u, k, high).start()

                @pl.when(k == n - 1)
                def _():
                    place = y_at(d, u, n - 1, row, high)
                    hop(d, u, n - 1, stage.at[d, u, 1, pl.ds(0, high)], place).start()
                    own_copy(d, u, row, high).start()

        @pl.when(k >= n)
        def _():
            for d in (0, 1):
                place = y_at(d, u, k, row, high)
                hop(d, u, k - 1, place, place).wait()

                @pl.when(k == n)
                def _():
                    own_copy(d, u, row, high).wait()

                @pl.when(k < HOPS)
                def _():
                    hop(d, u, k, place, place).start()

    def events(low, high_end, row, high):
        lax.fori_loop(low, high_end, lambda e, _: (event(e, row, high), 0)[1], 0)

    def one_pass(p, count, before, more):
        high = count // n

        @pl.loop(0, UP)
        def _(s):
            slot = lax.rem(p + s, 2)

            @pl.when(s < UP - 1)
            def _():
                start_up(s + 1, 1 - slot)

            @pl.when(s == UP - 1)
            def _():
                down_copy(0, 1 - slot).start()

            for copy in up_copies(s, slot):
                copy.wait()
            both = jnp.dot(x_buf[pl.ds(0, count), :], w_buf[slot], preferred_element_type=F32)
            cols = pl.ds(pl.multiple_of(s * tile, 128), tile)
            hid[pl.ds(0, count), cols] = (jax.nn.silu(both[:, :tile]) * both[:, tile:]).astype(BF16)
            before(s)

        @pl.loop(0, DOWN)
        def _(u):
            slot = lax.rem(p + UP + u, 2)

            @pl.when(u < DOWN - 1)
            def _():
                down_copy(u + 1, 1 - slot).start()

            @pl.when(u == DOWN - 1)
            def _():
                more(1 - slot)

            down_copy(u, slot).wait()
            out = jnp.dot(hid[pl.ds(0, count), :], w_buf[slot, pl.ds(0, units), :], preferred_element_type=F32)
            term[u, 0, pl.ds(0, count), :] = out[:, :half]
            term[u, 1, pl.ds(0, count), :] = out[:, half:]
            first_hop(u, high)
            before(u + UP)

    x_copy(0, few).start()
    start_up(0, 0)
    pl.semaphore_wait(barrier, 2)

    @pl.loop(0, SMALL)
    def _(p):
        x_copy(p * few, few).wait()

        def before(t):
            @pl.when(p > 0)
            def _():
                events(EVENTS * t // STEPS, EVENTS * (t + 1) // STEPS, (p - 1) * few, few // n)

        def more(slot):
            start_up(0, slot)

            @pl.when(p < SMALL - 1)
            def _():
                x_copy((p + 1) * few, few).start()

            @pl.when(p == SMALL - 1)
            def _():
                x_copy(SMALL * few, many).start()

        one_pass(p, few, before, more)

    @pl.loop(0, BIG)
    def _(q):
        row = SMALL * few + q * many
        x_copy(row, many).wait()

        def before(t):
            @pl.when((q == 0) & (t < HOPS))
            def _():
                events(DOWN * t, DOWN * (t + 1), (SMALL - 1) * few, few // n)

            @pl.when(q > 0)
            def _():
                events(EVENTS * t // STEPS, EVENTS * (t + 1) // STEPS, row - many, many // n)

        def more(slot):
            @pl.when(q < BIG - 1)
            def _():
                start_up(0, slot)
                x_copy(row + many, many).start()

        one_pass(SMALL + q, many, before, more)

    events(0, EVENTS, SMALL * few + (BIG - 1) * many, many // n)


PIECES = 8


def copy_kernel(y_hbm, out_hbm, buf, in_sem, out_sem):
    high = y_hbm.shape[0] // PIECES
    into = [pltpu.make_async_copy(y_hbm.at[pl.ds(i * high, high)], buf.at[i], in_sem.at[i]) for i in range(PIECES)]
    back = [pltpu.make_async_copy(buf.at[i], out_hbm.at[pl.ds(i * high, high)], out_sem.at[i]) for i in range(PIECES)]
    for copy in into:
        copy.start()
    for i in range(PIECES):
        into[i].wait()
        back[i].start()
    for copy in back:
        copy.wait()


def solution(mesh):
    n = mesh.shape["tp"]

    def step(x, w_gate, w_up, w_down):
        rows, dim = x.shape
        units = w_gate.shape[1]
        many, wide, tile = rows // 4, dim // DOWN, units // UP
        half, high = wide // 2, rows // 4 // n
        anywhere = pl.BlockSpec(memory_space=pl.ANY)
        y = pl.pallas_call(
            functools.partial(block_kernel, n),
            out_shape=jax.ShapeDtypeStruct((rows, dim), BF16),
            in_specs=[anywhere] * 4,
            out_specs=anywhere,
            scratch_shapes=[
                pltpu.VMEM((2, dim, max(wide, 2 * tile)), BF16),
                pltpu.VMEM((many, dim), BF16),
                pltpu.VMEM((many, units), BF16),
                pltpu.VMEM((DOWN, 2, many, half), F32),
                pltpu.VMEM((2, DOWN, 2, high, half), BF16),
                pltpu.VMEM((2, DOWN, n - 1, high, half), BF16),
                pltpu.SemaphoreType.DMA((2, 2)),
                pltpu.SemaphoreType.DMA,
                pltpu.SemaphoreType.DMA((2, DOWN)),
                pltpu.SemaphoreType.DMA((2, DOWN, HOPS)),
                pltpu.SemaphoreType.DMA((2, DOWN, HOPS)),
            ],
            compiler_params=pltpu.CompilerParams(
                collective_id=0, has_side_effects=True, vmem_limit_bytes=67043328
            ),
            name="block",
        )(x, w_gate, w_up, w_down)
        return pl.pallas_call(
            copy_kernel,
            out_shape=jax.ShapeDtypeStruct((rows, dim), BF16),
            in_specs=[anywhere],
            out_specs=anywhere,
            scratch_shapes=[
                pltpu.VMEM((PIECES, rows // PIECES, dim), BF16),
                pltpu.SemaphoreType.DMA((PIECES,)),
                pltpu.SemaphoreType.DMA((PIECES,)),
            ],
            compiler_params=pltpu.CompilerParams(vmem_limit_bytes=40 << 20),
            name="place",
        )(y)

    return jax.shard_map(
        step,
        mesh=mesh,
        in_specs=(P("dp", None), P(None, "tp"), P(None, "tp"), P("tp", None)),
        out_specs=P("dp", None),
        check_vma=False,
    )
```

time: 726 us -> 451 us (0.62)
  Pallas kernels: 0 us -> 450 us
  waiting for transfers between devices: 358 us -> 0 us
  matrix products: 337 us -> 0 us
  local copies, waits for them, and re-layouts: 17.3 us -> 0 us
  between operations: 13.4 us -> 0.17 us
    pallas_call x0 -> x2, Pallas kernels: none -> 450 us  [the longest x1 436 us: step(): pl.pallas_call(functools.partial(block_kernel, n), out_shape=jax.ShapeDty...]
    psum x1 -> x0, waiting for transfers between devices: 358 us -> none  [step(): return lax.psum(term, 'tp')]
    dot_general x3 -> x0, matrix products: 337 us -> none  [the longest x1 117 us: step(): up = jnp.dot(x, w_up, preferred_element_type=jnp.float32)]
    unnamed x1 -> x0, local copies, waits for them, and re-layouts: 17.3 us -> none
  transfers between devices with their start and end apart: 1 -> 0, of which waited for: 1 -> 0; matrix products, arithmetic and copies ran while one was open for 0% -> 0% of each run, Pallas kernels for 0% -> 0%
where the time goes in v1:
time: 451 us; the launch traced here: 450 us
  Pallas kernels  450 us (100%)
    pallas_call x1, Pallas kernels, step(): pl.pallas_call(functools.partial(block_kernel, n), out_shape=jax.ShapeDty...  436 us
    pallas_call x1, Pallas kernels, step(): pl.pallas_call(copy_kernel, out_shape=jax.ShapeDtypeStruct((rows, dim), B...  14.7 us

profile of v1, /device:TPU:112, one launch (start us, length us, event | category | flops | bytes accessed | tf_op | source)
XLA Modules:
  0.0 450.4 jit_solution(14012703139816923572)
XLA Ops:
  0.0 435.5 %block.1.y_hbm = bf16[2048,5120]{1,0:T(8,128)(2,1)} custom-call(bf16[2048,5120]{1,0:T(8,128)(2,1)} %x_hbm.1, bf16[5120,4480]{1,0:T(8,128)(2,1)} %wg_hbm.1, bf16[5120,4480]{1,0:T(8,128)(2,1)} %wu_hbm.1, bf16[4480,5120]{1,0:T(8,128)(2,1)} %wd_hbm.1), custom_call_target="tpu_custom_call" | custom-call | tf_op jit(solution)/shard_map/block/pallas_call | solution.py:241
  435.5 14.7 %place.1 = bf16[2048,5120]{1,0:T(8,128)(2,1)} custom-call(bf16[2048,5120]{1,0:T(8,128)(2,1)} %block.1.y_hbm), custom_call_target="tpu_custom_call" | custom-call | tf_op jit(solution)/shard_map/place/pallas_call | solution.py:264

commit v2 on v1

v2 whole, which is shorter than its diff:
```python
import functools

import jax
import jax.numpy as jnp
from jax import lax
from jax.experimental import pallas as pl
from jax.experimental.pallas import tpu as pltpu
from jax.sharding import PartitionSpec as P

MESH = pl.DeviceIdType.MESH
F32, BF16 = jnp.float32, jnp.bfloat16

SECTIONS = ((1, 4), (5, 5), (1, 3))
PASSES = sum(times for times, _ in SECTIONS)
LARGEST = max(size for _, size in SECTIONS)
SLOTS = 3
UP, DOWN = 7, 4
STEPS = UP + DOWN
HOPS = 6
PLAN = {
    1: ((1, 0),), 2: ((1, 1),), 3: ((2, 0),), 4: ((1, 2), (1, 3), (2, 1)), 5: ((2, 2), (3, 0)), 6: ((2, 3), (3, 1)),
    7: ((4, 0), (3, 2)), 8: ((3, 3), (4, 1)), 9: ((5, 0), (4, 2)), 10: ((4, 3), (5, 1)), 11: ((5, 2),),
    12: ((6, 0), (5, 3)), 13: ((6, 2),), 14: ((6, 1), (6, 3)),
}


def block_kernel(
    n, x_hbm, wg_hbm, wu_hbm, wd_hbm, y_hbm,
    w_buf, x_buf, hid, term, stage, got,
    w_sem, x_sem, o_sem, send_sem, recv_sem,
):
    rows, dim = x_hbm.shape
    units = wg_hbm.shape[1]
    wide = dim // DOWN
    half = wide // 2
    tile = units // UP
    part = rows // sum(times * size for times, size in SECTIONS)

    me = lax.axis_index("tp")
    group = lax.axis_index("dp")
    peers = (lax.rem(me + 1, n), lax.rem(me + n - 1, n))

    barrier = pltpu.get_barrier_semaphore()
    for peer in peers:
        pl.semaphore_signal(barrier, inc=1, device_id=(group, peer), device_id_type=MESH)

    def up_copies(s, slot):
        cols = pl.ds(pl.multiple_of(s * tile, 128), tile)
        return (
            pltpu.make_async_copy(wg_hbm.at[:, cols], w_buf.at[slot, :, pl.ds(0, tile)], w_sem.at[slot, 0]),
            pltpu.make_async_copy(wu_hbm.at[:, cols], w_buf.at[slot, :, pl.ds(tile, tile)], w_sem.at[slot, 1]),
        )

    def down_copy(s, slot):
        cols = pl.ds(pl.multiple_of(s * wide, 128), wide)
        return pltpu.make_async_copy(wd_hbm.at[:, cols], w_buf.at[slot, pl.ds(0, units), pl.ds(0, wide)], w_sem.at[slot, 0])

    def start_up(s, slot):
        for copy in up_copies(s, slot):
            copy.start()

    def x_copy(row, count):
        return pltpu.make_async_copy(x_hbm.at[pl.ds(pl.multiple_of(row, 16), count)], x_buf.at[pl.ds(0, count)], x_sem)

    def block_at(d, k):
        return lax.rem(me + 2 * n - 1 - k, n) if d == 0 else lax.rem(me + 1 + k, n)

    def y_at(d, u, k, row, high):
        start = pl.multiple_of(row + block_at(d, k) * high, 16)
        return y_hbm.at[pl.ds(start, high), pl.ds(pl.multiple_of(u * wide + d * half, 128), half)]

    def hop(d, u, k, src, dst):
        return pltpu.make_async_remote_copy(
            src_ref=src, dst_ref=dst,
            send_sem=send_sem.at[d, u, k], recv_sem=recv_sem.at[d, u, k],
            device_id=(group, peers[d]), device_id_type=MESH,
        )

    def partial_hop(d, u, k, high):
        return hop(d, u, k, stage.at[d, u, k % 2, pl.ds(0, high)], got.at[d, u, k, pl.ds(0, high)])

    def own_copy(d, u, row, high):
        return pltpu.make_async_copy(stage.at[d, u, 1, pl.ds(0, high)], y_at(d, u, n - 1, row, high), o_sem.at[d, u])

    def mine(d, u, k, high):
        return term[u, d, pl.ds(pl.multiple_of(block_at(d, k) * high, 16), high), :]

    def first_hop(u, high):
        for d in (0, 1):
            stage[d, u, 0, pl.ds(0, high), :] = mine(d, u, 0, high).astype(BF16)
            partial_hop(d, u, 0, high).start()

    def event(k, u, row, high):
        for d in (0, 1):
            if k < n:
                partial_hop(d, u, k - 1, high).wait()
                total = got[d, u, k - 1, pl.ds(0, high), :].astype(F32) + mine(d, u, k, high)
                stage[d, u, k % 2, pl.ds(0, high), :] = total.astype(BF16)
                if k < n - 1:
                    partial_hop(d, u, k, high).start()
                else:
                    hop(d, u, k, stage.at[d, u, k % 2, pl.ds(0, high)], y_at(d, u, k, row, high)).start()
                    own_copy(d, u, row, high).start()
            else:
                place = y_at(d, u, k, row, high)
                hop(d, u, k - 1, place, place).wait()
                if k == n:
                    own_copy(d, u, row, high).wait()
                if k < HOPS:
                    hop(d, u, k, place, place).start()

    def events(after, row, high):
        for k, u in PLAN.get(after, ()):
            event(k, u, row, high)

    x_copy(0, SECTIONS[0][1] * part).start()
    start_up(0, 0)
    start_up(1, 1)
    pl.semaphore_wait(barrier, 2)

    def section(i, first_pass, first_row):
        times, size = SECTIONS[i]
        count = size * part
        high = count // n
        final = i == len(SECTIONS) - 1

        @pl.loop(0, times)
        def _(p):
            row = first_row + p * count
            step = STEPS * (first_pass + p)

            def last_pass_events(t):
                @pl.when(p > 0)
                def _():
                    events(t + DOWN, row - count, high)

                if i > 0:
                    before = SECTIONS[i - 1][1] * part

                    @pl.when(p == 0)
                    def _():
                        events(t + DOWN, row - before, before // n)

            x_copy(row, count).wait()

            @pl.loop(0, UP)
            def _(s):
                slot = lax.rem(step + s, SLOTS)
                ahead = lax.rem(slot + 2, SLOTS)

                @pl.when(s < UP - 2)
                def _():
                    start_up(s + 2, ahead)

                @pl.when(s >= UP - 2)
                def _():
                    down_copy(s + 2 - UP, ahead).start()

                for copy in up_copies(s, slot):
                    copy.wait()
                both = jnp.dot(x_buf[pl.ds(0, count), :], w_buf[slot], preferred_element_type=F32)
                cols = pl.ds(pl.multiple_of(s * tile, 128), tile)
                hid[pl.ds(0, count), cols] = (jax.nn.silu(both[:, :tile]) * both[:, tile:]).astype(BF16)
                for t in range(UP):

                    @pl.when(s == t)
                    def _():
                        last_pass_events(t)

            @pl.loop(0, DOWN)
            def _(u):
                slot = lax.rem(step + UP + u, SLOTS)
                ahead = lax.rem(slot + 2, SLOTS)
                more = p < times - 1 if final else True

                @pl.when(u < DOWN - 2)
                def _():
                    down_copy(u + 2, ahead).start()

                @pl.when((u >= DOWN - 2) & more)
                def _():
                    start_up(u + 2 - DOWN, ahead)

                @pl.when((u == 0) & (p < times - 1))
                def _():
                    x_copy(row + count, count).start()

                if not final:

                    @pl.when((u == 0) & (p == times - 1))
                    def _():
                        x_copy(row + count, SECTIONS[i + 1][1] * part).start()

                down_copy(u, slot).wait()
                out = jnp.dot(hid[pl.ds(0, count), :], w_buf[slot, pl.ds(0, units), :], preferred_element_type=F32)
                term[u, 0, pl.ds(0, count), :] = out[:, :half]
                term[u, 1, pl.ds(0, count), :] = out[:, half:]
                first_hop(u, high)
                for t in range(DOWN):

                    @pl.when(u == t)
                    def _():
                        last_pass_events(UP + t)
                        events(t, row, high)

        return first_pass + times, first_row + times * count

    place = (0, 0)
    for i in range(len(SECTIONS)):
        place = section(i, *place)
    count = SECTIONS[-1][1] * part
    for after in range(DOWN, max(PLAN) + 1):
        events(after, rows - count, count // n)


PIECES = 8


def copy_kernel(y_hbm, out_hbm, buf, in_sem, out_sem):
    high = y_hbm.shape[0] // PIECES
    into = [pltpu.make_async_copy(y_hbm.at[pl.ds(i * high, high)], buf.at[i], in_sem.at[i]) for i in range(PIECES)]
    back = [pltpu.make_async_copy(buf.at[i], out_hbm.at[pl.ds(i * high, high)], out_sem.at[i]) for i in range(PIECES)]
    for copy in into:
        copy.start()
    for copy in into:
        copy.wait()
    for copy in back:
        copy.start()
    for copy in back:
        copy.wait()


def solution(mesh):
    n = mesh.shape["tp"]

    def step(x, w_gate, w_up, w_down):
        rows, dim = x.shape
        units = w_gate.shape[1]
        part = rows // sum(times * size for times, size in SECTIONS)
        count, wide, tile = LARGEST * part, dim // DOWN, units // UP
        half, high = wide // 2, count // n
        anywhere = pl.BlockSpec(memory_space=pl.ANY)
        y = pl.pallas_call(
            functools.partial(block_kernel, n),
            out_shape=jax.ShapeDtypeStruct((rows, dim), BF16),
            in_specs=[anywhere] * 4,
            out_specs=anywhere,
            scratch_shapes=[
                pltpu.VMEM((SLOTS, dim, max(wide, 2 * tile)), BF16),
                pltpu.VMEM((count, dim), BF16),
                pltpu.VMEM((count, units), BF16),
                pltpu.VMEM((DOWN, 2, count, half), F32),
                pltpu.VMEM((2, DOWN, 2, high, half), BF16),
                pltpu.VMEM((2, DOWN, n - 1, high, half), BF16),
                pltpu.SemaphoreType.DMA((SLOTS, 2)),
                pltpu.SemaphoreType.DMA,
                pltpu.SemaphoreType.DMA((2, DOWN)),
                pltpu.SemaphoreType.DMA((2, DOWN, HOPS)),
                pltpu.SemaphoreType.DMA((2, DOWN, HOPS)),
            ],
            compiler_params=pltpu.CompilerParams(
                collective_id=0, has_side_effects=True, vmem_limit_bytes=67043328
            ),
            name="block",
        )(x, w_gate, w_up, w_down)
        return pl.pallas_call(
            copy_kernel,
            out_shape=jax.ShapeDtypeStruct((rows, dim), BF16),
            in_specs=[anywhere],
            out_specs=anywhere,
            scratch_shapes=[
                pltpu.VMEM((PIECES, rows // PIECES, dim), BF16),
                pltpu.SemaphoreType.DMA((PIECES,)),
                pltpu.SemaphoreType.DMA((PIECES,)),
            ],
            compiler_params=pltpu.CompilerParams(vmem_limit_bytes=40 << 20),
            name="place",
        )(y)

    return jax.shard_map(
        step,
        mesh=mesh,
        in_specs=(P("dp", None), P(None, "tp"), P(None, "tp"), P("tp", None)),
        out_specs=P("dp", None),
        check_vma=False,
    )
```

time: 451 us -> 403 us (0.89)
  Pallas kernels: 450 us -> 402 us
    pallas_call x1, Pallas kernels: 436 us -> 388 us  [step(): pl.pallas_call(functools.partial(block_kernel, n), out_shape=jax.ShapeDty...]
where the time goes in v2:
time: 403 us
  Pallas kernels  402 us (100%)
    pallas_call x1, Pallas kernels, step(): pl.pallas_call(functools.partial(block_kernel, n), out_shape=jax.ShapeDty...  388 us
    pallas_call x1, Pallas kernels, step(): pl.pallas_call(copy_kernel, out_shape=jax.ShapeDtypeStruct((rows, dim), B...  14.3 us

profile of v2, /device:TPU:112, one launch (start us, length us, event | category | flops | bytes accessed | tf_op | source)
XLA Modules:
  0.0 402.5 jit_solution(9845587212658627503)
XLA Ops:
  0.0 388.0 %block.1.y_hbm = bf16[2048,5120]{1,0:T(8,128)(2,1)} custom-call(bf16[2048,5120]{1,0:T(8,128)(2,1)} %x_hbm.1, bf16[5120,4480]{1,0:T(8,128)(2,1)} %wg_hbm.1, bf16[5120,4480]{1,0:T(8,128)(2,1)} %wu_hbm.1, bf16[4480,5120]{1,0:T(8,128)(2,1)} %wd_hbm.1), custom_call_target="tpu_custom_call" | custom-call | tf_op jit(solution)/shard_map/block/pallas_call | solution.py:243
  388.0 14.3 %place.1 = bf16[2048,5120]{1,0:T(8,128)(2,1)} custom-call(bf16[2048,5120]{1,0:T(8,128)(2,1)} %block.1.y_hbm), custom_call_target="tpu_custom_call" | custom-call | tf_op jit(solution)/shard_map/place/pallas_call | solution.py:266

commit v3 on v2

--- a/solution.py
+++ b/solution.py
@@ -13,7 +13,9 @@
 SECTIONS = ((1, 4), (5, 5), (1, 3))
 PASSES = sum(times for times, _ in SECTIONS)
 LARGEST = max(size for _, size in SECTIONS)
-SLOTS = 3
+SLOTS = 2
+LEAD = SLOTS - 1
+BLOCK_VMEM, PLACE_VMEM = 38 << 20, 8 << 20
 UP, DOWN = 7, 4
 STEPS = UP + DOWN
 HOPS = 6
@@ -25,9 +27,9 @@
 
 
 def block_kernel(
-    n, x_hbm, wg_hbm, wu_hbm, wd_hbm, y_hbm,
-    w_buf, x_buf, hid, term, stage, got,
-    w_sem, x_sem, o_sem, send_sem, recv_sem,
+    n, x_hbm, wg_hbm, wu_hbm, wd_hbm, y_hbm, w_buf,
+    x_buf, hid, term, stage, got,
+    w_sem, x_sem, o_sem, send_sem, recv_sem, hold_sem,
 ):
     rows, dim = x_hbm.shape
     units = wg_hbm.shape[1]
@@ -114,8 +116,8 @@
             event(k, u, row, high)
 
     x_copy(0, SECTIONS[0][1] * part).start()
-    start_up(0, 0)
-    start_up(1, 1)
+    for i in range(LEAD):
+        start_up(i, i)
     pl.semaphore_wait(barrier, 2)
 
     def section(i, first_pass, first_row):
@@ -146,15 +148,15 @@
             @pl.loop(0, UP)
             def _(s):
                 slot = lax.rem(step + s, SLOTS)
-                ahead = lax.rem(slot + 2, SLOTS)
-
-                @pl.when(s < UP - 2)
-                def _():
-                    start_up(s + 2, ahead)
-
-                @pl.when(s >= UP - 2)
-                def _():
-                    down_copy(s + 2 - UP, ahead).start()
+                ahead = lax.rem(slot + LEAD, SLOTS)
+
+                @pl.when(s < UP - LEAD)
+                def _():
+                    start_up(s + LEAD, ahead)
+
+                @pl.when(s >= UP - LEAD)
+                def _():
+                    down_copy(s + LEAD - UP, ahead).start()
 
                 for copy in up_copies(s, slot):
                     copy.wait()
@@ -170,16 +172,16 @@
             @pl.loop(0, DOWN)
             def _(u):
                 slot = lax.rem(step + UP + u, SLOTS)
-                ahead = lax.rem(slot + 2, SLOTS)
+                ahead = lax.rem(slot + LEAD, SLOTS)
                 more = p < times - 1 if final else True
 
-                @pl.when(u < DOWN - 2)
-                def _():
-                    down_copy(u + 2, ahead).start()
-
-                @pl.when((u >= DOWN - 2) & more)
-                def _():
-                    start_up(u + 2 - DOWN, ahead)
+                @pl.when(u < DOWN - LEAD)
+                def _():
+                    down_copy(u + LEAD, ahead).start()
+
+                @pl.when((u >= DOWN - LEAD) & more)
+                def _():
+                    start_up(u + LEAD - DOWN, ahead)
 
                 @pl.when((u == 0) & (p < times - 1))
                 def _():
@@ -209,23 +211,42 @@
     for i in range(len(SECTIONS)):
         place = section(i, *place)
     count = SECTIONS[-1][1] * part
+    ready = rows - count
+    copies = [
+        pltpu.make_async_copy(
+            y_hbm.at[pl.ds(0, ready), pl.ds(c * wide, wide)], held(w_buf, c, rows, ready, wide), hold_sem.at[c]
+        )
+        for c in range(DOWN)
+    ]
+    for copy in copies:
+        copy.start()
     for after in range(DOWN, max(PLAN) + 1):
         events(after, rows - count, count // n)
-
-
-PIECES = 8
-
-
-def copy_kernel(y_hbm, out_hbm, buf, in_sem, out_sem):
-    high = y_hbm.shape[0] // PIECES
-    into = [pltpu.make_async_copy(y_hbm.at[pl.ds(i * high, high)], buf.at[i], in_sem.at[i]) for i in range(PIECES)]
-    back = [pltpu.make_async_copy(buf.at[i], out_hbm.at[pl.ds(i * high, high)], out_sem.at[i]) for i in range(PIECES)]
-    for copy in into:
+    for copy in copies:
+        copy.wait()
+
+
+def held(w_buf, c, rows, ready, wide):
+    return w_buf.at[c // 2, pl.ds(c % 2 * rows, ready), pl.ds(0, wide)]
+
+
+def place_kernel(y_hbm, w_buf, out_hbm, last, in_sem, out_sem):
+    rows, dim = y_hbm.shape
+    wide = dim // DOWN
+    ready = rows - last.shape[0]
+    into = pltpu.make_async_copy(y_hbm.at[pl.ds(ready, rows - ready)], last, in_sem)
+    into.start()
+    back = [
+        pltpu.make_async_copy(
+            held(w_buf, c, rows, ready, wide), out_hbm.at[pl.ds(0, ready), pl.ds(c * wide, wide)], out_sem.at[c]
+        )
+        for c in range(DOWN)
+    ]
+    back.append(pltpu.make_async_copy(last, out_hbm.at[pl.ds(ready, rows - ready)], out_sem.at[DOWN]))
+    for copy in back[:-1]:
         copy.start()
-    for copy in into:
-        copy.wait()
-    for copy in back:
-        copy.start()
+    into.wait()
+    back[-1].start()
     for copy in back:
         copy.wait()
 
@@ -240,13 +261,14 @@
         count, wide, tile = LARGEST * part, dim // DOWN, units // UP
         half, high = wide // 2, count // n
         anywhere = pl.BlockSpec(memory_space=pl.ANY)
-        y = pl.pallas_call(
+        weights = (SLOTS, dim, max(wide, 2 * tile))
+        in_vmem = pl.BlockSpec(memory_space=pltpu.VMEM)
+        y, kept = pl.pallas_call(
             functools.partial(block_kernel, n),
-            out_shape=jax.ShapeDtypeStruct((rows, dim), BF16),
+            out_shape=(jax.ShapeDtypeStruct((rows, dim), BF16), pltpu.VMEM(weights, BF16)),
             in_specs=[anywhere] * 4,
-            out_specs=anywhere,
+            out_specs=(anywhere, in_vmem),
             scratch_shapes=[
-                pltpu.VMEM((SLOTS, dim, max(wide, 2 * tile)), BF16),
                 pltpu.VMEM((count, dim), BF16),
                 pltpu.VMEM((count, units), BF16),
                 pltpu.VMEM((DOWN, 2, count, half), F32),
@@ -257,25 +279,26 @@
                 pltpu.SemaphoreType.DMA((2, DOWN)),
                 pltpu.SemaphoreType.DMA((2, DOWN, HOPS)),
                 pltpu.SemaphoreType.DMA((2, DOWN, HOPS)),
+                pltpu.SemaphoreType.DMA((DOWN,)),
             ],
             compiler_params=pltpu.CompilerParams(
-                collective_id=0, has_side_effects=True, vmem_limit_bytes=67043328
+                collective_id=0, has_side_effects=True, vmem_limit_bytes=BLOCK_VMEM
             ),
             name="block",
         )(x, w_gate, w_up, w_down)
         return pl.pallas_call(
-            copy_kernel,
+            place_kernel,
             out_shape=jax.ShapeDtypeStruct((rows, dim), BF16),
-            in_specs=[anywhere],
+            in_specs=[anywhere, anywhere],
             out_specs=anywhere,
             scratch_shapes=[
-                pltpu.VMEM((PIECES, rows // PIECES, dim), BF16),
-                pltpu.SemaphoreType.DMA((PIECES,)),
-                pltpu.SemaphoreType.DMA((PIECES,)),
+                pltpu.VMEM((SECTIONS[-1][1] * part, dim), BF16),
+                pltpu.SemaphoreType.DMA,
+                pltpu.SemaphoreType.DMA((DOWN + 1,)),
             ],
-            compiler_params=pltpu.CompilerParams(vmem_limit_bytes=40 << 20),
+            compiler_params=pltpu.CompilerParams(vmem_limit_bytes=PLACE_VMEM),
             name="place",
-        )(y)
+        )(y, pltpu.with_memory_space_constraint(kept, pltpu.VMEM))
 
     return jax.shard_map(
         step,

time: 403 us -> 409 us (1.015)
  local copies, waits for them, and re-layouts: 0 us -> 6.96 us
    unnamed x0 -> x2, local copies, waits for them, and re-layouts: none -> 6.96 us
where the time goes in v3:
time: 409 us; the launch traced here: 408 us
  Pallas kernels  401 us (98%)
  local copies, waits for them, and re-layouts  6.96 us (2%)
    pallas_call x1, Pallas kernels, step(): pl.pallas_call(functools.partial(block_kernel, n), out_shape=(jax.ShapeDt...  394 us

profile of v3, /device:TPU:112, one launch (start us, length us, event | category | flops | bytes accessed | tf_op | source)
XLA Modules:
  0.0 408.3 jit_solution(10564982479098936666)
XLA Ops:
  0.0 393.7 %block.1 = (bf16[2048,5120]{1,0:T(8,128)(2,1)}, bf16[2,5120,1280]{2,1,0:T(8,128)(2,1)S(1)}) custom-call(bf16[2048,5120]{1,0:T(8,128)(2,1)} %x_hbm.1, bf16[5120,4480]{1,0:T(8,128)(2,1)} %wg_hbm.1, bf16[5120,4480]{1,0:T(8,128)(2,1)} %wu_hbm.1, bf16[4480,5120]{1,0:T(8,128)(2,1)} %wd_hbm.1), custom_call_target="tpu_custom_call" | custom-call | tf_op jit(solution)/shard_map/block/pallas_call | solution.py:266
  393.7 0.0 copy-start
  393.7 7.0 %copy-done = bf16[2048,5120]{1,0:T(8,128)(2,1)S(1)} copy-done((bf16[2048,5120]{1,0:T(8,128)(2,1)S(1)}, bf16[2048,5120]{1,0:T(8,128)(2,1)}, u32[]{:S(2)}) %copy-start) | copy-done | bytes 20971544
  400.6 7.5 %place.1 = bf16[2048,5120]{1,0:T(8,128)(2,1)} custom-call(bf16[2048,5120]{1,0:T(8,128)(2,1)S(1)} %copy-done, bf16[2,5120,1280]{2,1,0:T(8,128)(2,1)S(1)} %get-tuple-element.8.w_buf), custom_call_target="tpu_custom_call" | custom-call | tf_op jit(solution)/shard_map/place/pallas_call | solution.py:289
Async XLA Ops:
  393.7 7.0 %copy-start = (bf16[2048,5120]{1,0:T(8,128)(2,1)S(1)}, bf16[2048,5120]{1,0:T(8,128)(2,1)}, u32[]{:S(2)}) copy-start(bf16[2048,5120]{1,0:T(8,128)(2,1)} %get-tuple-element.7.y_hbm) | copy-start | bytes 62914564
